TPU v7x, 512 devices: a whole 4x8x8 slice. The times are simulated.
512 devices in a mesh: energy: 64 (over y, z), block: 4 (over x), role: 2 (over core).
Axes of the slice: x: 4, y: 8, z: 8, core: 2. Of those that a mesh axis runs over, the one named last changes fastest.
Arguments:
- sigma_in: float32 [2, 128, 4, 128, 128], P(None, ('energy', 'role'), 'block'), may hold values from -0.009 to 0.009
- hamiltonian: float32 [4, 128, 128], P('block'), may hold values from -0.5 to 0.5
- coupling: float32 [4, 128, 128], P('block'), may hold values from -0.25 to 0.25
- coulomb: float32 [4, 16384], P('block', ('energy', 'role')), may hold values from 0.2 to 1
- pattern: int32 [2, 4, 4, 4], P(None, 'block'), may hold values 0 or 1
- offsets: int32 [16], replicated, may hold values from 0 to 63
Outputs:
- green: float32 [2, 128, 4, 128, 128], P(None, ('energy', 'role'), 'block')
- sigma_out: float32 [2, 128, 4, 128, 128], P(None, ('energy', 'role'), 'block')
All inputs are finite; a program needn't handle non-finite values. No bound on the sum of `pattern` on one device may be relied on, other than what follows from the above.
Results may differ from a plain program's by a relative error of at most 0.0003.
Values sent between devices are 32-bit elements; how exact they have to be, the bound alone decides.
A program may use at most 64 MiB of HBM per device.

v0:
```python
import functools

import jax
import jax.numpy as jnp
from jax import lax
from jax.experimental import pallas as pl
from jax.experimental.pallas import tpu as pltpu
from jax.sharding import PartitionSpec as P

TILE = 32
ETA = 0.1
CONTACT = 0.5
HIGH = lax.Precision.HIGHEST
F32 = jnp.float32


def dot(a, b):
    return jnp.dot(a, b, precision=HIGH, preferred_element_type=F32)


def row_of(x, k):
    return jnp.broadcast_to(x[k : k + 1, :], (8, 128))


def column_of(x, k):
    return jnp.broadcast_to(x[:, k : k + 1], (8, 128))


def small_inverse(cols):
    row = lax.broadcasted_iota(jnp.int32, (8, 128), 0)
    for k in range(8):
        here = row == k
        pr, pi = row_of(cols[k][0], k), row_of(cols[k][1], k)
        r = 1.0 / (pr * pr + pi * pi)
        ir, ii = pr * r, -(pi * r)
        cr, ci = cols[k]
        tr = jnp.where(here, -ir, cr * ir - ci * ii)
        ti = jnp.where(here, -ii, cr * ii + ci * ir)
        new = []
        for j in range(8):
            if j == k:
                new.append((-tr, -ti))
                continue
            a, b = cols[j]
            ar, ai = row_of(a, k), row_of(b, k)
            za, zb = jnp.where(here, 0.0, a), jnp.where(here, 0.0, b)
            new.append((za - (tr * ar - ti * ai), zb - (tr * ai + ti * ar)))
        cols = new
    return cols


def panel_inverse(pr, pi, base):
    lane = lax.broadcasted_iota(jnp.int32, (8, 128), 1)
    row = lax.broadcasted_iota(jnp.int32, (8, 128), 0)
    for q in range(4):
        at = base + 8 * q
        inv = small_inverse([(column_of(pr[q], at + j), column_of(pi[q], at + j)) for j in range(8)])
        inside = (lane >= at) & (lane < at + 8)
        sr = jnp.where(inside, jnp.where(lane - at == row, 1.0, 0.0), pr[q])
        si = jnp.where(inside, 0.0, pi[q])
        nr = ni = None
        for j in range(8):
            a, b = row_of(sr, j), row_of(si, j)
            er, ei = inv[j]
            xr, xi = er * a - ei * b, er * b + ei * a
            nr, ni = (xr, xi) if nr is None else (nr + xr, ni + xi)
        rows = [(row_of(nr, j), row_of(ni, j)) for j in range(8)]
        for i in range(4):
            if i == q:
                continue
            ar, ai = jnp.where(inside, 0.0, pr[i]), jnp.where(inside, 0.0, pi[i])
            for j in range(8):
                cr, ci = column_of(pr[i], at + j), column_of(pi[i], at + j)
                ar = ar - (cr * rows[j][0] - ci * rows[j][1])
                ai = ai - (cr * rows[j][1] + ci * rows[j][0])
            pr[i], pi[i] = ar, ai
        pr[q], pi[q] = nr, ni
    return pr, pi


def inverses(matrices):
    lane = lax.broadcasted_iota(jnp.int32, (96, 128), 1)
    state = [[[part[32 * s : 32 * s + 32] for s in range(4)] for part in m] for m in matrices]
    for p in range(4):
        base = 32 * p
        others = [(p + 1) % 4, (p + 2) % 4, (p + 3) % 4]
        panels = []
        for xr, xi in state:
            a = [xr[p][8 * i : 8 * i + 8] for i in range(4)]
            b = [xi[p][8 * i : 8 * i + 8] for i in range(4)]
            a, b = panel_inverse(a, b, base)
            panels.append((jnp.concatenate(a, 0), jnp.concatenate(b, 0)))
        following = []
        for (xr, xi), (nr, ni) in zip(state, panels):
            old_r = jnp.concatenate([xr[o] for o in others], 0)
            old_i = jnp.concatenate([xi[o] for o in others], 0)
            left = jnp.concatenate([old_r[:, base : base + 32], old_i[:, base : base + 32]], 1)
            right = jnp.concatenate([jnp.concatenate([nr, ni], 1), jnp.concatenate([-ni, nr], 1)], 0)
            change = dot(left, right)
            inside = (lane >= base) & (lane < base + 32)
            new_r = jnp.where(inside, 0.0, old_r) - change[:, :128]
            new_i = jnp.where(inside, 0.0, old_i) - change[:, 128:]
            yr, yi = [None] * 4, [None] * 4
            for t, o in enumerate(others):
                yr[o], yi[o] = new_r[32 * t : 32 * t + 32], new_i[32 * t : 32 * t + 32]
            yr[p], yi[p] = nr, ni
            following.append((yr, yi))
        state = following
    return [(jnp.concatenate(a, 0), jnp.concatenate(b, 0)) for a, b in state]


def complex_dot(a, b):
    left = jnp.concatenate(a, 1)
    right = jnp.concatenate([jnp.concatenate([b[0], b[1]], 1), jnp.concatenate([-b[1], b[0]], 1)], 0)
    whole = dot(left, right)
    return whole[:, :128], whole[:, 128:]


def real_left(k, g):
    whole = dot(k, jnp.concatenate(g, 1))
    return whole[:, :128], whole[:, 128:]


def real_right(g, k):
    whole = dot(jnp.concatenate(g, 0), k)
    return whole[:128], whole[128:]


def minus(a, b):
    return a[0] - b[0], a[1] - b[1]


def solve_kernel(x_ref, o_ref):
    position = lax.axis_index("block")
    forward = position >= 2
    first = jnp.where(forward, 0, 3)
    second = jnp.where(forward, 1, 2)
    third = jnp.where(forward, 2, 1)
    fourth = jnp.where(forward, 3, 0)
    near = jnp.where(forward, 0, 2)
    far = jnp.where(forward, 2, 0)

    def both(index, plain):
        k = x_ref[index, 2]
        kt = k.T
        return jnp.where(plain, k, kt), jnp.where(plain, kt, k)

    k1, k1t = both(near, forward)
    k2, k2t = both(1, forward)
    k3, k3t = both(far, jnp.logical_not(forward))
    ga, gd = inverses([(x_ref[first, 0], x_ref[first, 1]), (x_ref[fourth, 0], x_ref[fourth, 1])])
    sb = minus((x_ref[second, 0], x_ref[second, 1]), real_right(real_left(k1t, ga), k1))
    (gb,) = inverses([sb])
    gd_k3 = real_right(gd, k3)
    k3t_gd = real_left(k3t, gd)
    sc = minus((x_ref[third, 0], x_ref[third, 1]), real_right(k3t_gd, k3))
    sc = minus(sc, real_right(real_left(k2t, gb), k2))
    (gc,) = inverses([sc])
    back = complex_dot(complex_dot(gd_k3, gc), k3t_gd)
    inner = (position == 1) | (position == 2)
    o_ref[0] = jnp.where(inner, gc[0], gd[0] + back[0])
    o_ref[1] = jnp.where(inner, gc[1], gd[1] + back[1])


def screen_kernel(energies, count, offsets_ref, v_ref, weight_ref, o_ref, padded, polar):
    padded[:, :energies] = jnp.zeros((2, energies, 128), F32)
    padded[:, energies:] = v_ref[...]
    factor = 6.0 / energies / (2.0 * 3.141592653589793)

    def polarize(w, carry):
        start = energies - offsets_ref[w]
        mr, mi = padded[0, pl.ds(start, energies), :], padded[1, pl.ds(start, energies), :]
        vr, vi = v_ref[0], v_ref[1]
        polar[0, pl.ds(w, 1), :] = factor * jnp.sum(vr * mr - vi * mi, axis=0, keepdims=True)
        polar[1, pl.ds(w, 1), :] = factor * jnp.sum(vr * mi + vi * mr, axis=0, keepdims=True)
        return carry

    lax.fori_loop(0, count, polarize, 0)
    weight = weight_ref[...]
    scale = weight * weight * (1.0 / count)
    rows = 64
    for n in range(0, energies, rows):

        def interact(w, total):
            start = energies - offsets_ref[w] + n
            mr, mi = padded[0, pl.ds(start, rows), :], padded[1, pl.ds(start, rows), :]
            pr, pi = polar[0, pl.ds(w, 1), :], polar[1, pl.ds(w, 1), :]
            return total[0] + (mr * pr - mi * pi), total[1] + (mr * pi + mi * pr)

        zero = jnp.zeros((rows, 128), F32)
        tr, ti = lax.fori_loop(0, count, interact, (zero, zero))
        o_ref[0, n : n + rows] = tr * scale
        o_ref[1, n : n + rows] = ti * scale


def in_vmem():
    return pl.BlockSpec(memory_space=pltpu.VMEM)


def expand(tiles):
    big = jnp.broadcast_to(tiles[:, None, :, None], (tiles.shape[0], TILE, tiles.shape[1], TILE))
    return big.reshape(tiles.shape[0] * TILE, tiles.shape[1] * TILE).astype(F32)


def body(sigma_in, hamiltonian, coupling, coulomb, pattern, offsets):
    width = hamiltonian.shape[-1]
    position = lax.axis_index("block")
    blocks = lax.axis_size("block")
    groups = lax.axis_size("energy") * lax.axis_size("role")
    place = lax.axis_index("energy") * lax.axis_size("role") + lax.axis_index("role")
    identity = jnp.eye(width, dtype=F32)
    energy = -3.0 + 6.0 * place.astype(F32) / groups
    onsite = hamiltonian[0] * expand(pattern[0, 0])
    onsite = 0.5 * (onsite + onsite.T)
    k = coupling[0]
    ends = jnp.where(position == blocks - 1, 1.0, 0.0)
    square = jnp.dot(k.T, k, precision=HIGH, preferred_element_type=F32)
    real = energy * identity - onsite - sigma_in[0, 0, 0]
    imag = ETA * identity - sigma_in[1, 0, 0] + ends * CONTACT * square
    mine = jnp.stack([real, imag, k])
    every = lax.all_to_all(jnp.broadcast_to(mine[None], (blocks, *mine.shape)), "block", 0, 0, tiled=True)
    green = pl.pallas_call(
        solve_kernel,
        out_shape=jax.ShapeDtypeStruct((2, width, width), F32),
        in_specs=[in_vmem()],
        out_specs=in_vmem(),
        cost_estimate=pl.CostEstimate(flops=2_000_000_000, bytes_accessed=900_000, transcendentals=0),
    )(every)
    values = lax.all_to_all(green, ("energy", "role"), split_axis=1, concat_axis=1, tiled=True)
    tiles = lax.dynamic_slice_in_dim(pattern[1, 0], place // TILE, 1, 0)
    weight = coulomb * jnp.repeat(tiles, TILE, axis=1).astype(F32)
    elements = pl.pallas_call(
        functools.partial(screen_kernel, groups, offsets.shape[0]),
        out_shape=jax.ShapeDtypeStruct((2, groups, width), F32),
        in_specs=[pl.BlockSpec(memory_space=pltpu.SMEM), in_vmem(), in_vmem()],
        out_specs=in_vmem(),
        scratch_shapes=[pltpu.VMEM((2, 2 * groups, width), F32), pltpu.VMEM((2, offsets.shape[0], width), F32)],
    )(offsets, values, weight)
    returned = lax.all_to_all(elements, ("energy", "role"), split_axis=1, concat_axis=1, tiled=True)
    return green[:, None, None], returned[:, None, None]


def solution(mesh):
    spread = P(None, ("energy", "role"), "block", None, None)
    in_specs = (
        spread,
        P("block", None, None),
        P("block", None, None),
        P("block", ("energy", "role")),
        P(None, "block", None, None),
        P(),
    )
    return jax.shard_map(body, mesh=mesh, in_specs=in_specs, out_specs=(spread, spread), check_vma=False)
```

profile of v0, /device:TPU:1, one launch (start us, length us, event | category | flops | bytes accessed | tf_op | source)
XLA Modules:
  0.0 102.0 jit_solution(11881331402208590791)
XLA Ops:
  0.6 0.0 copy-start.2
  0.6 0.7 copy-done.2
  1.3 0.1 copy.14
  1.4 0.9 copy.13
  2.4 0.1 broadcast_in_dim.20
  2.5 0.2 convert_element_type.35
  2.6 0.0 copy-start.1
  2.7 0.0 copy-start
  2.7 0.1 copy.15
  2.8 0.8 copy-done.1
  3.5 0.0 copy-done
  3.5 0.3 fusion.1
  3.9 0.1 broadcast_in_dim.21
  4.0 13.1 %all_to_all.15.x_ref = f32[4,3,128,128]{3,2,1,0:T(8,128)} all-to-all(f32[4,3,128,128]{3,2,1,0:T(8,128)S(1)} %broadcast_in_dim.21), channel_id=1, replica_groups=mesh['energy'=64,'block'=4,'role'=2] {'block'}, dimensions={0} | all-to-all | bytes 1572864 | tf_op jit(solution)/shard_map/all_to_all | solution.py:221
  17.0 26.0 %shard_map.77 = f32[2,128,128]{2,1,0:T(8,128)} custom-call(f32[4,3,128,128]{3,2,1,0:T(8,128)} %all_to_all.15.x_ref), custom_call_target="tpu_custom_call" | custom-call | flops 2000000000 | bytes 900000 | tf_op jit(solution)/shard_map/pallas_call | solution.py:222
  43.0 1.7 %copy.16 = f32[2,128,128]{2,0,1:T(2,128)} copy(f32[2,128,128]{2,1,0:T(8,128)} %shard_map.77) | data formatting | bytes 262144 | tf_op jit(solution)/shard_map/pallas_call | solution.py:222
  44.7 21.8 %all-to-all-start.1 = ((f32[2,128,128]{2,0,1:T(2,128)}), f32[2,128,128]{2,0,1:T(2,128)S(1)}, u32[]{:S(2)}, u32[]{:S(2)}) async-start(f32[2,128,128]{2,0,1:T(2,128)} %copy.16), calls=%async_computation.1 | async-start | bytes 262144 | tf_op jit(solution)/shard_map/all_to_all | solution.py:229
  66.6 0.1 broadcast_in_dim.23
  66.6 0.0 copy-start.3
  66.6 0.1 convert_element_type.38
  66.7 0.6 copy-done.3
  67.3 0.5 mul.47.weight_ref
  67.8 11.0 %all-to-all-done.1 = f32[2,128,128]{2,0,1:T(2,128)S(1)} async-done(((f32[2,128,128]{2,0,1:T(2,128)}), f32[2,128,128]{2,0,1:T(2,128)S(1)}, u32[]{:S(2)}, u32[]{:S(2)}) %all-to-all-start.1) | async-done | bytes 131104 | tf_op jit(solution)/shard_map/all_to_all | solution.py:229
  78.8 0.7 copy.17.v_ref
  79.5 2.8 %shard_map.78 = f32[2,128,128]{2,1,0:T(8,128)} custom-call(s32[16]{0:T(128)} %offsets_ref.1, f32[2,128,128]{2,1,0:T(8,128)} %copy.17.v_ref, f32[1,128]{1,0:T(1,128)} %mul.47.weight_ref), custom_call_target="tpu_custom_call" | custom-call | tf_op jit(solution)/shard_map/pallas_call | solution.py:232
  82.2 1.0 copy.18
  83.2 18.1 %all_to_all.16 = f32[2,128,128]{2,0,1:T(2,128)S(1)} all-to-all(f32[2,128,128]{2,0,1:T(2,128)S(1)} %copy.18), channel_id=1, replica_groups=mesh['energy'=64,'block'=4,'role'=2] {'energy','role'}, dimensions={1} | all-to-all | bytes 262144 | tf_op jit(solution)/shard_map/all_to_all | solution.py:239
  101.3 0.7 copy.20
  (5 shorter events, 0.1 us)
Async XLA Ops:
  0.6 0.7 copy-start.2
  2.6 0.9 copy-start.1
  2.7 0.9 copy-start
  44.7 34.1 %all-to-all-start.1 = ((f32[2,128,128]{2,0,1:T(2,128)}), f32[2,128,128]{2,0,1:T(2,128)S(1)}, u32[]{:S(2)}, u32[]{:S(2)}) async-start(f32[2,128,128]{2,0,1:T(2,128)} %copy.16), calls=%async_computation.1 | async-start | bytes 262144 | tf_op jit(solution)/shard_map/all_to_all | solution.py:229
  66.6 0.7 copy-start.3
where the time goes:
time: 102 us
  blocking collectives  31.2 us (31%)
  Pallas kernels  28.8 us (28%)
  starting transfers between devices  21.8 us (21%)
  waiting for transfers between devices  11 us (11%)
  local copies, waits for them, and re-layouts  7.6 us (7%)
    pallas_call x1, Pallas kernels, body(): pl.pallas_call(solve_kernel, out_shape=jax.ShapeDtypeStruct((2, width, wi...  26 us
    all_to_all x1, starting transfers between devices, body(): lax.all_to_all(green, ('energy', 'role'), split_axis=1, concat_axis=1, ti...  21.8 us
    all_to_all x1, blocking collectives, body(): lax.all_to_all(elements, ('energy', 'role'), split_axis=1, concat_axis=1,...  18.1 us
    all_to_all x1, blocking collectives, body(): lax.all_to_all(jnp.broadcast_to(mine[None], (blocks, *mine.shape)), 'bloc...  13.1 us
    all_to_all x1, waiting for transfers between devices, body(): lax.all_to_all(green, ('energy', 'role'), split_axis=1, concat_axis=1, ti...  11 us
    unnamed x10, local copies, waits for them, and re-layouts  3.61 us
    pallas_call x1, Pallas kernels, body(): pl.pallas_call(functools.partial(screen_kernel, groups, offsets.shape[0])...  2.76 us
  transfers between devices with their start and end apart: 1, of which 1 were waited for; matrix products, arithmetic and copies ran while one was open for 1% of the time, Pallas kernels for 0%

commit v1 on v0

--- a/solution.py
+++ b/solution.py
@@ -162,62 +162,148 @@
     o_ref[1] = jnp.where(inner, gc[1], gd[1] + back[1])
 
 
-def screen_kernel(energies, count, offsets_ref, v_ref, weight_ref, o_ref, padded, polar):
-    padded[:, :energies] = jnp.zeros((2, energies, 128), F32)
-    padded[:, energies:] = v_ref[...]
+def tile_row(tiles_ref, p, i, rows, width):
+    lane = lax.broadcasted_iota(jnp.int32, (rows, width), 1)
+    strip = jnp.zeros((rows, width), F32)
+    for j in range(width // TILE):
+        strip = jnp.where((lane >= TILE * j) & (lane < TILE * j + TILE), tiles_ref[p, 0, i, j].astype(F32), strip)
+    return strip
+
+
+def exchange(place, cur, mid, out, send, recv, base):
+    slow, fast, row_partner, slow_partner = place
+    started = []
+
+    def push(source, target, index, device):
+        copy = pltpu.make_async_remote_copy(
+            src_ref=source,
+            dst_ref=target,
+            send_sem=send.at[base + index],
+            recv_sem=recv.at[base + index],
+            device_id=device,
+            device_id_type=pl.DeviceIdType.MESH,
+        )
+        copy.start()
+        return copy
+
+    fasts = sorted(range(1, 16), key=lambda s: -min(s, 16 - s))
+    slows = sorted(range(1, 8), key=lambda s: -min(s, 8 - s))
+    one, two = [], []
+    for s in fasts:
+        t, device = row_partner(s)
+        one.append(push(cur.at[0, :, t, :], mid.at[0, :, fast, :], s, device))
+    for s in slows:
+        t, device = slow_partner(s)
+        two.append(push(cur.at[1, t], mid.at[1, slow], 16 + s, device))
+    mid[0, :, pl.ds(fast, 1), :] = cur[0, :, pl.ds(fast, 1), :]
+    mid[1, pl.ds(slow, 1)] = cur[1, pl.ds(slow, 1)]
+    for copy in two:
+        copy.wait()
+    for s in fasts:
+        t, device = row_partner(s)
+        started.append(push(mid.at[1, :, t, :], out.at[1, :, fast, :], 24 + s, device))
+    for copy in one:
+        copy.wait()
+    for s in slows:
+        t, device = slow_partner(s)
+        started.append(push(mid.at[0, t], out.at[0, slow], 40 + s, device))
+    out[1, :, pl.ds(fast, 1), :] = mid[1, :, pl.ds(fast, 1), :]
+    out[0, pl.ds(slow, 1)] = mid[0, pl.ds(slow, 1)]
+    for copy in started:
+        copy.wait()
+
+
+def screen_kernel(count, offsets_ref, tiles_ref, v_ref, coulomb_ref, o_ref, mid, padded, polar, done, mid_back, send, recv):
+    energies = 128
     factor = 6.0 / energies / (2.0 * 3.141592653589793)
+    e, c = lax.axis_index("energy"), lax.axis_index("role")
+    slow, z = e // 8, lax.rem(e, 8)
+    fast = 2 * z + c
+
+    def row_partner(s):
+        t = lax.rem(fast + s, 16)
+        return t, {"energy": slow * 8 + t // 2, "role": lax.rem(t, 2)}
+
+    def slow_partner(s):
+        t = lax.rem(slow + s, 8)
+        return t, {"energy": t * 8 + z, "role": c}
+
+    place = slow, fast, row_partner, slow_partner
+    barrier = pltpu.get_barrier_semaphore()
+    for partner, others in ((row_partner, 16), (slow_partner, 8)):
+        for s in range(1, others):
+            pl.semaphore_signal(barrier, inc=1, device_id=partner(s)[1], device_id_type=pl.DeviceIdType.MESH)
+    padded[:, :8] = jnp.zeros((2, 8, 16, 128), F32)
+    pl.semaphore_wait(barrier, 22)
+    exchange(place, v_ref, mid, padded.at[:, 8:], send, recv, 0)
+    flat = padded.reshape(2, 2 * energies, 128)
+    result = done.reshape(2, energies, 128)
 
     def polarize(w, carry):
         start = energies - offsets_ref[w]
-        mr, mi = padded[0, pl.ds(start, energies), :], padded[1, pl.ds(start, energies), :]
-        vr, vi = v_ref[0], v_ref[1]
+        mr, mi = flat[0, pl.ds(start, energies), :], flat[1, pl.ds(start, energies), :]
+        vr, vi = flat[0, energies:, :], flat[1, energies:, :]
         polar[0, pl.ds(w, 1), :] = factor * jnp.sum(vr * mr - vi * mi, axis=0, keepdims=True)
         polar[1, pl.ds(w, 1), :] = factor * jnp.sum(vr * mi + vi * mr, axis=0, keepdims=True)
         return carry
 
     lax.fori_loop(0, count, polarize, 0)
-    weight = weight_ref[...]
+    weight = coulomb_ref[...] * tile_row(tiles_ref, 1, (2 * e + c) // TILE, 1, 128)
     scale = weight * weight * (1.0 / count)
     rows = 64
     for n in range(0, energies, rows):
 
         def interact(w, total):
             start = energies - offsets_ref[w] + n
-            mr, mi = padded[0, pl.ds(start, rows), :], padded[1, pl.ds(start, rows), :]
+            mr, mi = flat[0, pl.ds(start, rows), :], flat[1, pl.ds(start, rows), :]
             pr, pi = polar[0, pl.ds(w, 1), :], polar[1, pl.ds(w, 1), :]
             return total[0] + (mr * pr - mi * pi), total[1] + (mr * pi + mi * pr)
 
         zero = jnp.zeros((rows, 128), F32)
         tr, ti = lax.fori_loop(0, count, interact, (zero, zero))
-        o_ref[0, n : n + rows] = tr * scale
-        o_ref[1, n : n + rows] = ti * scale
+        result[0, n : n + rows] = tr * scale
+        result[1, n : n + rows] = ti * scale
+    exchange(place, done, mid_back, o_ref, send, recv, 48)
+
+
+def system_kernel(tiles_ref, sigma_ref, hamiltonian_ref, coupling_ref, o_ref):
+    position = lax.axis_index("block")
+    place = lax.axis_index("energy") * lax.axis_size("role") + lax.axis_index("role")
+    width = hamiltonian_ref.shape[-1]
+    row = lax.broadcasted_iota(jnp.int32, (width, width), 0)
+    column = lax.broadcasted_iota(jnp.int32, (width, width), 1)
+    strips = [tile_row(tiles_ref, 0, i, TILE, width) for i in range(width // TILE)]
+    masked = hamiltonian_ref[0] * jnp.concatenate(strips, 0)
+    onsite = 0.5 * (masked + masked.T)
+    groups = lax.axis_size("energy") * lax.axis_size("role")
+    energy = -3.0 + 6.0 * place.astype(F32) / groups
+    k = coupling_ref[0]
+    diagonal = row == column
+    o_ref[0] = jnp.where(diagonal, energy, 0.0) - onsite - sigma_ref[0, 0, 0]
+    bare = jnp.where(diagonal, ETA, 0.0) - sigma_ref[1, 0, 0]
+    last = position == lax.axis_size("block") - 1
+    o_ref[1] = bare + jnp.where(last, CONTACT * dot(k.T, k), 0.0)
+    o_ref[2] = k
 
 
 def in_vmem():
     return pl.BlockSpec(memory_space=pltpu.VMEM)
 
 
-def expand(tiles):
-    big = jnp.broadcast_to(tiles[:, None, :, None], (tiles.shape[0], TILE, tiles.shape[1], TILE))
-    return big.reshape(tiles.shape[0] * TILE, tiles.shape[1] * TILE).astype(F32)
+def in_smem():
+    return pl.BlockSpec(memory_space=pltpu.SMEM)
 
 
 def body(sigma_in, hamiltonian, coupling, coulomb, pattern, offsets):
     width = hamiltonian.shape[-1]
-    position = lax.axis_index("block")
     blocks = lax.axis_size("block")
-    groups = lax.axis_size("energy") * lax.axis_size("role")
-    place = lax.axis_index("energy") * lax.axis_size("role") + lax.axis_index("role")
-    identity = jnp.eye(width, dtype=F32)
-    energy = -3.0 + 6.0 * place.astype(F32) / groups
-    onsite = hamiltonian[0] * expand(pattern[0, 0])
-    onsite = 0.5 * (onsite + onsite.T)
-    k = coupling[0]
-    ends = jnp.where(position == blocks - 1, 1.0, 0.0)
-    square = jnp.dot(k.T, k, precision=HIGH, preferred_element_type=F32)
-    real = energy * identity - onsite - sigma_in[0, 0, 0]
-    imag = ETA * identity - sigma_in[1, 0, 0] + ends * CONTACT * square
-    mine = jnp.stack([real, imag, k])
+    count = offsets.shape[0]
+    mine = pl.pallas_call(
+        system_kernel,
+        out_shape=jax.ShapeDtypeStruct((3, width, width), F32),
+        in_specs=[in_smem(), in_vmem(), in_vmem(), in_vmem()],
+        out_specs=in_vmem(),
+    )(pattern, sigma_in, hamiltonian, coupling)
     every = lax.all_to_all(jnp.broadcast_to(mine[None], (blocks, *mine.shape)), "block", 0, 0, tiled=True)
     green = pl.pallas_call(
         solve_kernel,
@@ -226,18 +312,25 @@
         out_specs=in_vmem(),
         cost_estimate=pl.CostEstimate(flops=2_000_000_000, bytes_accessed=900_000, transcendentals=0),
     )(every)
-    values = lax.all_to_all(green, ("energy", "role"), split_axis=1, concat_axis=1, tiled=True)
-    tiles = lax.dynamic_slice_in_dim(pattern[1, 0], place // TILE, 1, 0)
-    weight = coulomb * jnp.repeat(tiles, TILE, axis=1).astype(F32)
-    elements = pl.pallas_call(
-        functools.partial(screen_kernel, groups, offsets.shape[0]),
-        out_shape=jax.ShapeDtypeStruct((2, groups, width), F32),
-        in_specs=[pl.BlockSpec(memory_space=pltpu.SMEM), in_vmem(), in_vmem()],
+    planes = (2, 8, 16, width)
+    screened = pl.pallas_call(
+        functools.partial(screen_kernel, count),
+        out_shape=jax.ShapeDtypeStruct(planes, F32),
+        in_specs=[in_smem(), in_smem(), in_vmem(), in_vmem()],
         out_specs=in_vmem(),
-        scratch_shapes=[pltpu.VMEM((2, 2 * groups, width), F32), pltpu.VMEM((2, offsets.shape[0], width), F32)],
-    )(offsets, values, weight)
-    returned = lax.all_to_all(elements, ("energy", "role"), split_axis=1, concat_axis=1, tiled=True)
-    return green[:, None, None], returned[:, None, None]
+        scratch_shapes=[
+            pltpu.VMEM(planes, F32),
+            pltpu.VMEM((2, 16, 16, width), F32),
+            pltpu.VMEM((2, count, width), F32),
+            pltpu.VMEM(planes, F32),
+            pltpu.VMEM(planes, F32),
+            pltpu.SemaphoreType.DMA((96,)),
+            pltpu.SemaphoreType.DMA((96,)),
+        ],
+        compiler_params=pltpu.CompilerParams(collective_id=1, has_side_effects=True),
+    )(offsets, pattern, green.reshape(planes), coulomb)
+    spread = (2, 1, 1, width, width)
+    return green.reshape(spread), screened.reshape(spread)
 
 
 def solution(mesh):

time: 102 us -> 85.7 us (0.84)
  Pallas kernels: 28.8 us -> 69.2 us
  starting transfers between devices: 21.8 us -> 0 us
  blocking collectives: 31.2 us -> 13.1 us
  waiting for transfers between devices: 11 us -> 0 us
  local copies, waits for them, and re-layouts: 7.6 us -> 2.56 us
    pallas_call x1 -> x2, Pallas kernels: 2.76 us -> 43.2 us  [the longest x1 41.3 us: body(): pl.pallas_call(functools.partial(screen_kernel, count), out_shape=jax.Sha...]
    all_to_all x1 -> x0, starting transfers between devices: 21.8 us -> none  [body(): lax.all_to_all(green, ('energy', 'role'), split_axis=1, concat_axis=1, ti...]
    all_to_all x1 -> x0, blocking collectives: 18.1 us -> none  [body(): lax.all_to_all(elements, ('energy', 'role'), split_axis=1, concat_axis=1,...]
    all_to_all x1 -> x0, waiting for transfers between devices: 11 us -> none  [body(): lax.all_to_all(green, ('energy', 'role'), split_axis=1, concat_axis=1, ti...]
    pallas_call x2 -> x0, local copies, waits for them, and re-layouts: 2.67 us -> none  [the longest x1 1.66 us: body(): pl.pallas_call(solve_kernel, out_shape=jax.ShapeDtypeStruct((2, width, wi...]
    unnamed x10 -> x1, local copies, waits for them, and re-layouts: 3.61 us -> 1.57 us
  transfers between devices with their start and end apart: 1 -> 0, of which waited for: 1 -> 0; matrix products, arithmetic and copies ran while one was open for 1% -> 0% of each run, Pallas kernels for 0% -> 0%
where the time goes in v1:
time: 85.7 us; the launch traced here: 85.5 us
  Pallas kernels  69.2 us (81%)
  blocking collectives  13.1 us (15%)
  local copies, waits for them, and re-layouts  2.56 us (3%)
    pallas_call x1, Pallas kernels, body(): pl.pallas_call(functools.partial(screen_kernel, count), out_shape=jax.Sha...  41.3 us
    pallas_call x1, Pallas kernels, body(): pl.pallas_call(solve_kernel, out_shape=jax.ShapeDtypeStruct((2, width, wi...  26 us
    all_to_all x1, blocking collectives, body(): lax.all_to_all(jnp.broadcast_to(mine[None], (blocks, *mine.shape)), 'bloc...  13.1 us
    pallas_call x1, Pallas kernels, body(): pl.pallas_call(system_kernel, out_shape=jax.ShapeDtypeStruct((3, width, w...  1.89 us

profile of v1, /device:TPU:1, one launch (start us, length us, event | category | flops | bytes accessed | tf_op | source)
XLA Modules:
  0.0 85.5 jit_solution(14906878828004040789)
XLA Ops:
  0.6 1.9 %shard_map.77 = f32[3,128,128]{2,1,0:T(8,128)} custom-call(s32[2,1,4,4]{3,2,1,0:T(4,128)} %tiles_ref.3, f32[2,1,1,128,128]{4,3,2,1,0:T(8,128)} %sigma_ref.1, f32[1,128,128]{2,1,0:T(8,128)} %hamiltonian_ref.1, f32[1,128,128]{2,1,0:T(8,128)} %coupling_ref.1), custom_call_target="tpu_custom_call" | custom-call | tf_op jit(solution)/shard_map/pallas_call | solution.py:301
  2.5 1.0 %broadcast_in_dim.2 = f32[4,3,128,128]{3,2,1,0:T(8,128)S(1)} broadcast(f32[3,128,128]{2,1,0:T(8,128)} %shard_map.77), dimensions={1,2,3} | broadcast | bytes 983040 | tf_op jit(solution)/shard_map/broadcast_in_dim | solution.py:307
  3.5 13.1 %all_to_all.5.x_ref = f32[4,3,128,128]{3,2,1,0:T(8,128)} all-to-all(f32[4,3,128,128]{3,2,1,0:T(8,128)S(1)} %broadcast_in_dim.2), channel_id=1, replica_groups=mesh['energy'=64,'block'=4,'role'=2] {'block'}, dimensions={0} | all-to-all | bytes 1572864 | tf_op jit(solution)/shard_map/all_to_all | solution.py:307
  16.6 26.0 %shard_map.78 = f32[2,128,128]{2,1,0:T(8,128)} custom-call(f32[4,3,128,128]{3,2,1,0:T(8,128)} %all_to_all.5.x_ref), custom_call_target="tpu_custom_call" | custom-call | flops 2000000000 | bytes 900000 | tf_op jit(solution)/shard_map/pallas_call | solution.py:308
  42.6 41.3 %shard_map.79 = f32[2,8,16,128]{3,2,1,0:T(8,128)} custom-call(s32[16]{0:T(128)} %offsets_ref.1, s32[2,1,4,4]{3,2,1,0:T(4,128)} %tiles_ref.3, f32[2,8,16,128]{3,2,1,0:T(8,128)} %bitcast.8, f32[1,128]{1,0:T(1,128)} %coulomb_ref.1), custom_call_target="tpu_custom_call" | custom-call | tf_op jit(solution)/shard_map/pallas_call | solution.py:316
  83.9 1.6 %copy.11 = f32[2,1,1,128,128]{4,3,2,1,0:T(8,128)} copy(f32[2,1,1,128,128]{4,3,2,1,0:T(8,128)} %bitcast.7) | data formatting | bytes 262144

commit v2 on v1

--- a/solution.py
+++ b/solution.py
@@ -26,84 +26,93 @@
     return jnp.broadcast_to(x[:, k : k + 1], (8, 128))
 
 
-def small_inverse(cols):
+def times(a, b):
+    return a[0] * b[0] - a[1] * b[1], a[0] * b[1] + a[1] * b[0]
+
+
+def pair_step(cols, panel, k):
     row = lax.broadcasted_iota(jnp.int32, (8, 128), 0)
-    for k in range(8):
-        here = row == k
-        pr, pi = row_of(cols[k][0], k), row_of(cols[k][1], k)
-        r = 1.0 / (pr * pr + pi * pi)
-        ir, ii = pr * r, -(pi * r)
-        cr, ci = cols[k]
-        tr = jnp.where(here, -ir, cr * ir - ci * ii)
-        ti = jnp.where(here, -ii, cr * ii + ci * ir)
-        new = []
-        for j in range(8):
-            if j == k:
-                new.append((-tr, -ti))
-                continue
-            a, b = cols[j]
-            ar, ai = row_of(a, k), row_of(b, k)
-            za, zb = jnp.where(here, 0.0, a), jnp.where(here, 0.0, b)
-            new.append((za - (tr * ar - ti * ai), zb - (tr * ai + ti * ar)))
-        cols = new
-    return cols
-
-
-def panel_inverse(pr, pi, base):
+    l = k + 1
+    at_k, at_l = row == k, row == l
+    both = at_k | at_l
+    ck, cl = cols[k], cols[l]
+    a = row_of(ck[0], k), row_of(ck[1], k)
+    b = row_of(cl[0], k), row_of(cl[1], k)
+    c = row_of(ck[0], l), row_of(ck[1], l)
+    d = row_of(cl[0], l), row_of(cl[1], l)
+    ad, bc = times(a, d), times(b, c)
+    er, ei = ad[0] - bc[0], ad[1] - bc[1]
+    r = 1.0 / (er * er + ei * ei)
+    kd, lc = times(ck, d), times(cl, c)
+    la, kb = times(cl, a), times(ck, b)
+    uk = tuple(jnp.where(at_k, -d[p], jnp.where(at_l, c[p], kd[p] - lc[p])) for p in (0, 1))
+    ul = tuple(jnp.where(at_k, b[p], jnp.where(at_l, -a[p], la[p] - kb[p])) for p in (0, 1))
+    inv = er * r, -(ei * r)
+    tk, tl = times(uk, inv), times(ul, inv)
+
+    def update(z):
+        x, y = z
+        u = times(tk, (row_of(x, k), row_of(y, k)))
+        v = times(tl, (row_of(x, l), row_of(y, l)))
+        return jnp.where(both, 0.0, x) - (u[0] + v[0]), jnp.where(both, 0.0, y) - (u[1] + v[1])
+
+    return [z if j <= l else update(z) for j, z in enumerate(cols)], update(panel)
+
+
+def panels_inverse(chains, base):
     lane = lax.broadcasted_iota(jnp.int32, (8, 128), 1)
     row = lax.broadcasted_iota(jnp.int32, (8, 128), 0)
+    chains = [(list(a), list(b)) for a, b in chains]
+    total = len(chains[0][0])
     for q in range(4):
         at = base + 8 * q
-        inv = small_inverse([(column_of(pr[q], at + j), column_of(pi[q], at + j)) for j in range(8)])
         inside = (lane >= at) & (lane < at + 8)
-        sr = jnp.where(inside, jnp.where(lane - at == row, 1.0, 0.0), pr[q])
-        si = jnp.where(inside, 0.0, pi[q])
-        nr = ni = None
-        for j in range(8):
-            a, b = row_of(sr, j), row_of(si, j)
-            er, ei = inv[j]
-            xr, xi = er * a - ei * b, er * b + ei * a
-            nr, ni = (xr, xi) if nr is None else (nr + xr, ni + xi)
-        rows = [(row_of(nr, j), row_of(ni, j)) for j in range(8)]
-        for i in range(4):
+        unit = jnp.where(lane - at == row, 1.0, 0.0)
+        work = []
+        for pr, pi in chains:
+            cols = [(column_of(pr[q], at + j), column_of(pi[q], at + j)) for j in range(8)]
+            work.append((cols, (jnp.where(inside, unit, pr[q]), jnp.where(inside, 0.0, pi[q]))))
+        for k in range(0, 8, 2):
+            work = [pair_step(cols, panel, k) for cols, panel in work]
+        rows = [[(row_of(n[0], j), row_of(n[1], j)) for j in range(8)] for _, n in work]
+        for i in [(q + 1 + i) % total for i in range(total)]:
             if i == q:
                 continue
-            ar, ai = jnp.where(inside, 0.0, pr[i]), jnp.where(inside, 0.0, pi[i])
-            for j in range(8):
-                cr, ci = column_of(pr[i], at + j), column_of(pi[i], at + j)
-                ar = ar - (cr * rows[j][0] - ci * rows[j][1])
-                ai = ai - (cr * rows[j][1] + ci * rows[j][0])
-            pr[i], pi[i] = ar, ai
-        pr[q], pi[q] = nr, ni
-    return pr, pi
+            for (pr, pi), own in zip(chains, rows):
+                terms = [times((column_of(pr[i], at + j), column_of(pi[i], at + j)), own[j]) for j in range(8)]
+                while len(terms) > 1:
+                    pairs = zip(terms[::2], terms[1::2])
+                    terms = [(m[0] + n[0], m[1] + n[1]) for m, n in pairs]
+                pr[i] = jnp.where(inside, 0.0, pr[i]) - terms[0][0]
+                pi[i] = jnp.where(inside, 0.0, pi[i]) - terms[0][1]
+        for (pr, pi), (_, n) in zip(chains, work):
+            pr[q], pi[q] = n
+    return chains
 
 
 def inverses(matrices):
-    lane = lax.broadcasted_iota(jnp.int32, (96, 128), 1)
-    state = [[[part[32 * s : 32 * s + 32] for s in range(4)] for part in m] for m in matrices]
+    lane = lax.broadcasted_iota(jnp.int32, (8, 128), 1)
+    state = [[[part[8 * s : 8 * s + 8] for s in range(16)] for part in m] for m in matrices]
     for p in range(4):
         base = 32 * p
-        others = [(p + 1) % 4, (p + 2) % 4, (p + 3) % 4]
-        panels = []
-        for xr, xi in state:
-            a = [xr[p][8 * i : 8 * i + 8] for i in range(4)]
-            b = [xi[p][8 * i : 8 * i + 8] for i in range(4)]
-            a, b = panel_inverse(a, b, base)
-            panels.append((jnp.concatenate(a, 0), jnp.concatenate(b, 0)))
+        own = [4 * p + i for i in range(4 if p == 3 else 5)]
+        others = [s % 16 for s in range(4 * p + len(own), 4 * p + 16)]
+        inside = (lane >= base) & (lane < base + 32)
+        panels = panels_inverse([([xr[s] for s in own], [xi[s] for s in own]) for xr, xi in state], base)
         following = []
         for (xr, xi), (nr, ni) in zip(state, panels):
             old_r = jnp.concatenate([xr[o] for o in others], 0)
             old_i = jnp.concatenate([xi[o] for o in others], 0)
             left = jnp.concatenate([old_r[:, base : base + 32], old_i[:, base : base + 32]], 1)
-            right = jnp.concatenate([jnp.concatenate([nr, ni], 1), jnp.concatenate([-ni, nr], 1)], 0)
+            fr, fi = jnp.concatenate(nr[:4], 0), jnp.concatenate(ni[:4], 0)
+            right = jnp.concatenate([jnp.concatenate([fr, fi], 1), jnp.concatenate([-fi, fr], 1)], 0)
             change = dot(left, right)
-            inside = (lane >= base) & (lane < base + 32)
-            new_r = jnp.where(inside, 0.0, old_r) - change[:, :128]
-            new_i = jnp.where(inside, 0.0, old_i) - change[:, 128:]
-            yr, yi = [None] * 4, [None] * 4
+            yr, yi = [None] * 16, [None] * 16
             for t, o in enumerate(others):
-                yr[o], yi[o] = new_r[32 * t : 32 * t + 32], new_i[32 * t : 32 * t + 32]
-            yr[p], yi[p] = nr, ni
+                yr[o] = jnp.where(inside, 0.0, xr[o]) - change[8 * t : 8 * t + 8, :128]
+                yi[o] = jnp.where(inside, 0.0, xi[o]) - change[8 * t : 8 * t + 8, 128:]
+            for t, o in enumerate(own):
+                yr[o], yi[o] = nr[t], ni[t]
             following.append((yr, yi))
         state = following
     return [(jnp.concatenate(a, 0), jnp.concatenate(b, 0)) for a, b in state]
@@ -130,7 +139,7 @@
     return a[0] - b[0], a[1] - b[1]
 
 
-def solve_kernel(x_ref, o_ref):
+def solve_kernel(x_ref, o_ref, again_ref):
     position = lax.axis_index("block")
     forward = position >= 2
     first = jnp.where(forward, 0, 3)
@@ -158,8 +167,10 @@
     (gc,) = inverses([sc])
     back = complex_dot(complex_dot(gd_k3, gc), k3t_gd)
     inner = (position == 1) | (position == 2)
-    o_ref[0] = jnp.where(inner, gc[0], gd[0] + back[0])
-    o_ref[1] = jnp.where(inner, gc[1], gd[1] + back[1])
+    for part in (0, 1):
+        value = jnp.where(inner, gc[part], gd[part] + back[part])
+        o_ref[part] = value
+        again_ref[part] = value
 
 
 def tile_row(tiles_ref, p, i, rows, width):
@@ -266,8 +277,19 @@
     exchange(place, done, mid_back, o_ref, send, recv, 48)
 
 
-def system_kernel(tiles_ref, sigma_ref, hamiltonian_ref, coupling_ref, o_ref):
+def gather_kernel(tiles, sigma, hamiltonian, coupling, o_ref, tiles_ref, sigma_ref, hamiltonian_ref, coupling_ref, local, send, recv):
+    count = 4
     position = lax.axis_index("block")
+    right, left = lax.rem(position + 1, count), lax.rem(position + count - 1, count)
+    barrier = pltpu.get_barrier_semaphore()
+    for neighbour in (left, right):
+        pl.semaphore_signal(barrier, inc=1, device_id={"block": neighbour}, device_id_type=pl.DeviceIdType.MESH)
+    pairs = (tiles, tiles_ref), (sigma, sigma_ref), (hamiltonian, hamiltonian_ref), (coupling, coupling_ref)
+    loads = [pltpu.make_async_copy(source, target, local.at[i]) for i, (source, target) in enumerate(pairs)]
+    for load in loads:
+        load.start()
+    for load in loads:
+        load.wait()
     place = lax.axis_index("energy") * lax.axis_size("role") + lax.axis_index("role")
     width = hamiltonian_ref.shape[-1]
     row = lax.broadcasted_iota(jnp.int32, (width, width), 0)
@@ -279,11 +301,36 @@
     energy = -3.0 + 6.0 * place.astype(F32) / groups
     k = coupling_ref[0]
     diagonal = row == column
-    o_ref[0] = jnp.where(diagonal, energy, 0.0) - onsite - sigma_ref[0, 0, 0]
+    real = jnp.where(diagonal, energy, 0.0) - onsite - sigma_ref[0, 0, 0]
     bare = jnp.where(diagonal, ETA, 0.0) - sigma_ref[1, 0, 0]
-    last = position == lax.axis_size("block") - 1
-    o_ref[1] = bare + jnp.where(last, CONTACT * dot(k.T, k), 0.0)
-    o_ref[2] = k
+    last = position == count - 1
+    o_ref[pl.ds(position, 1)] = jnp.stack([real, bare + jnp.where(last, CONTACT * dot(k.T, k), 0.0), k])[None]
+    pl.semaphore_wait(barrier, 2)
+    half = width // 2
+    upper, lower = pl.ds(0, half), pl.ds(half, half)
+
+    def push(owner, rows, index, device):
+        return pltpu.make_async_remote_copy(
+            src_ref=o_ref.at[owner, :, rows, :],
+            dst_ref=o_ref.at[owner, :, rows, :],
+            send_sem=send.at[index],
+            recv_sem=recv.at[index],
+            device_id={"block": device},
+            device_id_type=pl.DeviceIdType.MESH,
+        )
+
+    first = [push(position, upper, 0, right), push(position, lower, 1, left)]
+    second = [push(position, lower, 2, right), push(position, upper, 3, left)]
+    for copy in first + second:
+        copy.start()
+    onward = [push(left, upper, 4, right), push(right, lower, 5, left)]
+    for copy, following in zip(first, onward):
+        copy.wait_recv()
+        following.start()
+    for copy in first:
+        copy.wait_send()
+    for copy in second + onward:
+        copy.wait()
 
 
 def in_vmem():
@@ -296,21 +343,29 @@
 
 def body(sigma_in, hamiltonian, coupling, coulomb, pattern, offsets):
     width = hamiltonian.shape[-1]
-    blocks = lax.axis_size("block")
     count = offsets.shape[0]
-    mine = pl.pallas_call(
-        system_kernel,
-        out_shape=jax.ShapeDtypeStruct((3, width, width), F32),
-        in_specs=[in_smem(), in_vmem(), in_vmem(), in_vmem()],
+    every = pl.pallas_call(
+        gather_kernel,
+        out_shape=jax.ShapeDtypeStruct((4, 3, width, width), F32),
+        in_specs=[pl.BlockSpec(memory_space=pl.ANY)] * 4,
         out_specs=in_vmem(),
+        scratch_shapes=[
+            pltpu.SMEM(pattern.shape, pattern.dtype),
+            pltpu.VMEM(sigma_in.shape, F32),
+            pltpu.VMEM(hamiltonian.shape, F32),
+            pltpu.VMEM(coupling.shape, F32),
+            pltpu.SemaphoreType.DMA((4,)),
+            pltpu.SemaphoreType.DMA((6,)),
+            pltpu.SemaphoreType.DMA((6,)),
+        ],
+        compiler_params=pltpu.CompilerParams(collective_id=2, has_side_effects=True, vmem_limit_bytes=66_180_000),
     )(pattern, sigma_in, hamiltonian, coupling)
-    every = lax.all_to_all(jnp.broadcast_to(mine[None], (blocks, *mine.shape)), "block", 0, 0, tiled=True)
-    green = pl.pallas_call(
+    green, again = pl.pallas_call(
         solve_kernel,
-        out_shape=jax.ShapeDtypeStruct((2, width, width), F32),
+        out_shape=[jax.ShapeDtypeStruct((2, width, width), F32)] * 2,
         in_specs=[in_vmem()],
-        out_specs=in_vmem(),
-        cost_estimate=pl.CostEstimate(flops=2_000_000_000, bytes_accessed=900_000, transcendentals=0),
+        out_specs=[in_vmem()] * 2,
+        compiler_params=pltpu.CompilerParams(vmem_limit_bytes=24 << 20),
     )(every)
     planes = (2, 8, 16, width)
     screened = pl.pallas_call(
@@ -327,8 +382,8 @@
             pltpu.SemaphoreType.DMA((96,)),
             pltpu.SemaphoreType.DMA((96,)),
         ],
-        compiler_params=pltpu.CompilerParams(collective_id=1, has_side_effects=True),
-    )(offsets, pattern, green.reshape(planes), coulomb)
+        compiler_params=pltpu.CompilerParams(collective_id=1, has_side_effects=True, vmem_limit_bytes=8 << 20),
+    )(offsets, pattern, again.reshape(planes), coulomb)
     spread = (2, 1, 1, width, width)
     return green.reshape(spread), screened.reshape(spread)
 

time: 85.7 us -> 76.1 us (0.89)
  blocking collectives: 13.1 us -> 0 us
  Pallas kernels: 69.2 us -> 72.7 us
    all_to_all x1 -> x0, blocking collectives: 13.1 us -> none  [body(): lax.all_to_all(jnp.broadcast_to(mine[None], (blocks, *mine.shape)), 'bloc...]
    pallas_call x2, Pallas kernels: 27.9 us -> 34.3 us  [the longest x1 23 us: body(): pl.pallas_call(solve_kernel, out_shape=[jax.ShapeDtypeStruct((2, width, w...]
    pallas_call x1, Pallas kernels: 41.3 us -> 38.4 us  [body(): pl.pallas_call(functools.partial(screen_kernel, count), out_shape=jax.Sha...]
    broadcast_in_dim x1 -> x0, local copies, waits for them, and re-layouts: 0.99 us -> none  [body(): jnp.broadcast_to(mine[None], (blocks, *mine.shape))]
    unnamed x1 -> x9, local copies, waits for them, and re-layouts: 1.57 us -> 2.47 us
where the time goes in v2:
time: 76.1 us; the launch traced here: 75.8 us
  Pallas kernels  72.7 us (96%)
  local copies, waits for them, and re-layouts  2.47 us (3%)
    pallas_call x1, Pallas kernels, body(): pl.pallas_call(functools.partial(screen_kernel, count), out_shape=jax.Sha...  38.4 us
    pallas_call x1, Pallas kernels, body(): pl.pallas_call(solve_kernel, out_shape=[jax.ShapeDtypeStruct((2, width, w...  23 us
    pallas_call x1, Pallas kernels, body(): pl.pallas_call(gather_kernel, out_shape=jax.ShapeDtypeStruct((4, 3, width...  11.3 us
    unnamed x9, local copies, waits for them, and re-layouts  2.47 us

profile of v2, /device:TPU:1, one launch (start us, length us, event | category | flops | bytes accessed | tf_op | source)
XLA Modules:
  0.0 75.8 jit_solution(12221675555628490587)
XLA Ops:
  0.6 11.3 %shard_map.77.x_ref = f32[4,3,128,128]{3,2,1,0:T(8,128)} custom-call(s32[2,1,4,4]{3,2,1,0:T(4,128)} %tiles_ref.1, f32[2,1,1,128,128]{4,3,2,1,0:T(8,128)} %sigma.1, f32[1,128,128]{2,1,0:T(8,128)} %hamiltonian.1, f32[1,128,128]{2,1,0:T(8,128)} %coupling.1), custom_call_target="tpu_custom_call" | custom-call | tf_op jit(solution)/shard_map/pallas_call | solution.py:347
  11.9 0.0 copy-start
  11.9 1.1 %copy-done = f32[4,3,128,128]{3,2,1,0:T(8,128)S(1)} copy-done((f32[4,3,128,128]{3,2,1,0:T(8,128)S(1)}, f32[4,3,128,128]{3,2,1,0:T(8,128)}, u32[]{:S(2)}) %copy-start) | copy-done | bytes 786456
  13.1 23.0 %shard_map.78 = (f32[2,128,128]{2,1,0:T(8,128)}, f32[2,128,128]{2,1,0:T(8,128)S(1)}) custom-call(f32[4,3,128,128]{3,2,1,0:T(8,128)S(1)} %copy-done), custom_call_target="tpu_custom_call" | custom-call | tf_op jit(solution)/shard_map/pallas_call | solution.py:363
  36.1 0.0 copy-start.1
  36.1 0.0 copy-start.2
  36.1 0.0 copy-start.3
  36.1 0.7 copy-done.1
  36.8 0.0 copy-done.2
  36.8 0.0 copy-done.3
  36.8 38.4 %shard_map.79 = f32[2,8,16,128]{3,2,1,0:T(8,128)S(1)} custom-call(s32[16]{0:T(128)S(1)} %copy-done.2, s32[2,1,4,4]{3,2,1,0:T(4,128)S(1)} %copy-done.1, f32[2,8,16,128]{3,2,1,0:T(8,128)S(1)} %bitcast.8, f32[1,128]{1,0:T(1,128)S(1)} %copy-done.3), custom_call_target="tpu_custom_call" | custom-call | tf_op jit(solution)/shard_map/pallas_call | solution.py:371
  75.2 0.7 copy.11
Async XLA Ops:
  11.9 1.1 %copy-start = (f32[4,3,128,128]{3,2,1,0:T(8,128)S(1)}, f32[4,3,128,128]{3,2,1,0:T(8,128)}, u32[]{:S(2)}) copy-start(f32[4,3,128,128]{3,2,1,0:T(8,128)} %shard_map.77.x_ref) | copy-start | bytes 2359300
  36.1 0.7 copy-start.1
  36.1 0.7 copy-start.2
  36.1 0.7 copy-start.3

commit v3 on v2

--- a/solution.py
+++ b/solution.py
@@ -139,40 +139,6 @@
     return a[0] - b[0], a[1] - b[1]
 
 
-def solve_kernel(x_ref, o_ref, again_ref):
-    position = lax.axis_index("block")
-    forward = position >= 2
-    first = jnp.where(forward, 0, 3)
-    second = jnp.where(forward, 1, 2)
-    third = jnp.where(forward, 2, 1)
-    fourth = jnp.where(forward, 3, 0)
-    near = jnp.where(forward, 0, 2)
-    far = jnp.where(forward, 2, 0)
-
-    def both(index, plain):
-        k = x_ref[index, 2]
-        kt = k.T
-        return jnp.where(plain, k, kt), jnp.where(plain, kt, k)
-
-    k1, k1t = both(near, forward)
-    k2, k2t = both(1, forward)
-    k3, k3t = both(far, jnp.logical_not(forward))
-    ga, gd = inverses([(x_ref[first, 0], x_ref[first, 1]), (x_ref[fourth, 0], x_ref[fourth, 1])])
-    sb = minus((x_ref[second, 0], x_ref[second, 1]), real_right(real_left(k1t, ga), k1))
-    (gb,) = inverses([sb])
-    gd_k3 = real_right(gd, k3)
-    k3t_gd = real_left(k3t, gd)
-    sc = minus((x_ref[third, 0], x_ref[third, 1]), real_right(k3t_gd, k3))
-    sc = minus(sc, real_right(real_left(k2t, gb), k2))
-    (gc,) = inverses([sc])
-    back = complex_dot(complex_dot(gd_k3, gc), k3t_gd)
-    inner = (position == 1) | (position == 2)
-    for part in (0, 1):
-        value = jnp.where(inner, gc[part], gd[part] + back[part])
-        o_ref[part] = value
-        again_ref[part] = value
-
-
 def tile_row(tiles_ref, p, i, rows, width):
     lane = lax.broadcasted_iota(jnp.int32, (rows, width), 1)
     strip = jnp.zeros((rows, width), F32)
@@ -224,72 +190,10 @@
         copy.wait()
 
 
-def screen_kernel(count, offsets_ref, tiles_ref, v_ref, coulomb_ref, o_ref, mid, padded, polar, done, mid_back, send, recv):
-    energies = 128
-    factor = 6.0 / energies / (2.0 * 3.141592653589793)
-    e, c = lax.axis_index("energy"), lax.axis_index("role")
-    slow, z = e // 8, lax.rem(e, 8)
-    fast = 2 * z + c
-
-    def row_partner(s):
-        t = lax.rem(fast + s, 16)
-        return t, {"energy": slow * 8 + t // 2, "role": lax.rem(t, 2)}
-
-    def slow_partner(s):
-        t = lax.rem(slow + s, 8)
-        return t, {"energy": t * 8 + z, "role": c}
-
-    place = slow, fast, row_partner, slow_partner
-    barrier = pltpu.get_barrier_semaphore()
-    for partner, others in ((row_partner, 16), (slow_partner, 8)):
-        for s in range(1, others):
-            pl.semaphore_signal(barrier, inc=1, device_id=partner(s)[1], device_id_type=pl.DeviceIdType.MESH)
-    padded[:, :8] = jnp.zeros((2, 8, 16, 128), F32)
-    pl.semaphore_wait(barrier, 22)
-    exchange(place, v_ref, mid, padded.at[:, 8:], send, recv, 0)
-    flat = padded.reshape(2, 2 * energies, 128)
-    result = done.reshape(2, energies, 128)
-
-    def polarize(w, carry):
-        start = energies - offsets_ref[w]
-        mr, mi = flat[0, pl.ds(start, energies), :], flat[1, pl.ds(start, energies), :]
-        vr, vi = flat[0, energies:, :], flat[1, energies:, :]
-        polar[0, pl.ds(w, 1), :] = factor * jnp.sum(vr * mr - vi * mi, axis=0, keepdims=True)
-        polar[1, pl.ds(w, 1), :] = factor * jnp.sum(vr * mi + vi * mr, axis=0, keepdims=True)
-        return carry
-
-    lax.fori_loop(0, count, polarize, 0)
-    weight = coulomb_ref[...] * tile_row(tiles_ref, 1, (2 * e + c) // TILE, 1, 128)
-    scale = weight * weight * (1.0 / count)
-    rows = 64
-    for n in range(0, energies, rows):
-
-        def interact(w, total):
-            start = energies - offsets_ref[w] + n
-            mr, mi = flat[0, pl.ds(start, rows), :], flat[1, pl.ds(start, rows), :]
-            pr, pi = polar[0, pl.ds(w, 1), :], polar[1, pl.ds(w, 1), :]
-            return total[0] + (mr * pr - mi * pi), total[1] + (mr * pi + mi * pr)
-
-        zero = jnp.zeros((rows, 128), F32)
-        tr, ti = lax.fori_loop(0, count, interact, (zero, zero))
-        result[0, n : n + rows] = tr * scale
-        result[1, n : n + rows] = ti * scale
-    exchange(place, done, mid_back, o_ref, send, recv, 48)
-
-
-def gather_kernel(tiles, sigma, hamiltonian, coupling, o_ref, tiles_ref, sigma_ref, hamiltonian_ref, coupling_ref, local, send, recv):
-    count = 4
-    position = lax.axis_index("block")
-    right, left = lax.rem(position + 1, count), lax.rem(position + count - 1, count)
-    barrier = pltpu.get_barrier_semaphore()
-    for neighbour in (left, right):
-        pl.semaphore_signal(barrier, inc=1, device_id={"block": neighbour}, device_id_type=pl.DeviceIdType.MESH)
-    pairs = (tiles, tiles_ref), (sigma, sigma_ref), (hamiltonian, hamiltonian_ref), (coupling, coupling_ref)
-    loads = [pltpu.make_async_copy(source, target, local.at[i]) for i, (source, target) in enumerate(pairs)]
-    for load in loads:
-        load.start()
-    for load in loads:
-        load.wait()
+MESH = pl.DeviceIdType.MESH
+
+
+def build_system(position, tiles_ref, sigma_ref, hamiltonian_ref, coupling_ref, x_ref):
     place = lax.axis_index("energy") * lax.axis_size("role") + lax.axis_index("role")
     width = hamiltonian_ref.shape[-1]
     row = lax.broadcasted_iota(jnp.int32, (width, width), 0)
@@ -303,34 +207,172 @@
     diagonal = row == column
     real = jnp.where(diagonal, energy, 0.0) - onsite - sigma_ref[0, 0, 0]
     bare = jnp.where(diagonal, ETA, 0.0) - sigma_ref[1, 0, 0]
-    last = position == count - 1
-    o_ref[pl.ds(position, 1)] = jnp.stack([real, bare + jnp.where(last, CONTACT * dot(k.T, k), 0.0), k])[None]
-    pl.semaphore_wait(barrier, 2)
-    half = width // 2
-    upper, lower = pl.ds(0, half), pl.ds(half, half)
-
-    def push(owner, rows, index, device):
+    imag = bare + jnp.where(position == 3, CONTACT * dot(k.T, k), 0.0)
+    x_ref[pl.ds(position, 1)] = jnp.stack([real, imag])[None]
+
+
+def solve(position, x_ref, k_ref, couplings_arrived):
+    forward = position >= 2
+    first = jnp.where(forward, 0, 3)
+    second = jnp.where(forward, 1, 2)
+    third = jnp.where(forward, 2, 1)
+    fourth = jnp.where(forward, 3, 0)
+
+    def both(index, plain):
+        k = k_ref[index]
+        kt = k.T
+        return jnp.where(plain, k, kt), jnp.where(plain, kt, k)
+
+    ga, gd = inverses([(x_ref[first, 0], x_ref[first, 1]), (x_ref[fourth, 0], x_ref[fourth, 1])])
+    couplings_arrived()
+    k1, k1t = both(jnp.where(forward, 0, 2), forward)
+    k2, k2t = both(1, forward)
+    k3, k3t = both(jnp.where(forward, 2, 0), jnp.logical_not(forward))
+    sb = minus((x_ref[second, 0], x_ref[second, 1]), real_right(real_left(k1t, ga), k1))
+    (gb,) = inverses([sb])
+    gd_k3 = real_right(gd, k3)
+    k3t_gd = real_left(k3t, gd)
+    sc = minus((x_ref[third, 0], x_ref[third, 1]), real_right(k3t_gd, k3))
+    sc = minus(sc, real_right(real_left(k2t, gb), k2))
+    (gc,) = inverses([sc])
+    back = complex_dot(complex_dot(gd_k3, gc), k3t_gd)
+    inner = (position == 1) | (position == 2)
+    return [jnp.where(inner, gc[part], gd[part] + back[part]) for part in (0, 1)]
+
+
+def whole_kernel(
+    count,
+    offsets_ref,
+    tiles,
+    sigma,
+    hamiltonian,
+    coupling,
+    coulomb,
+    green_ref,
+    o_ref,
+    tiles_ref,
+    sigma_ref,
+    hamiltonian_ref,
+    coulomb_ref,
+    x_ref,
+    k_ref,
+    held,
+    mid,
+    padded,
+    polar,
+    done,
+    mid_back,
+    local,
+    ring_send,
+    ring_recv,
+    send,
+    recv,
+):
+    energies = 128
+    factor = 6.0 / energies / (2.0 * 3.141592653589793)
+    position = lax.axis_index("block")
+    e, c = lax.axis_index("energy"), lax.axis_index("role")
+    slow, z = e // 8, lax.rem(e, 8)
+    fast = 2 * z + c
+    right, opposite, left = [lax.rem(position + s, 4) for s in (1, 2, 3)]
+    pairs = (
+        (coupling, k_ref.at[pl.ds(position, 1)]),
+        (tiles, tiles_ref),
+        (sigma, sigma_ref),
+        (hamiltonian, hamiltonian_ref),
+        (coulomb, coulomb_ref),
+    )
+    loads = [pltpu.make_async_copy(source, target, local.at[i]) for i, (source, target) in enumerate(pairs)]
+    for load in loads:
+        load.start()
+
+    def row_partner(s):
+        t = lax.rem(fast + s, 16)
+        return t, {"energy": slow * 8 + t // 2, "role": lax.rem(t, 2)}
+
+    def slow_partner(s):
+        t = lax.rem(slow + s, 8)
+        return t, {"energy": t * 8 + z, "role": c}
+
+    place = slow, fast, row_partner, slow_partner
+    barrier = pltpu.get_barrier_semaphore()
+    for partner, others in ((row_partner, 16), (slow_partner, 8)):
+        for s in range(1, others):
+            pl.semaphore_signal(barrier, inc=1, device_id=partner(s)[1], device_id_type=MESH)
+    for block in (right, opposite, left):
+        pl.semaphore_signal(barrier, inc=1, device_id={"block": block}, device_id_type=MESH)
+    padded[:, :8] = jnp.zeros((2, 8, 16, 128), F32)
+    for load in loads:
+        load.wait()
+    build_system(position, tiles_ref, sigma_ref, hamiltonian_ref, k_ref.at[pl.ds(position, 1)], x_ref)
+    pl.semaphore_wait(barrier, 25)
+
+    def push(ref, index, block):
         return pltpu.make_async_remote_copy(
-            src_ref=o_ref.at[owner, :, rows, :],
-            dst_ref=o_ref.at[owner, :, rows, :],
-            send_sem=send.at[index],
-            recv_sem=recv.at[index],
-            device_id={"block": device},
-            device_id_type=pl.DeviceIdType.MESH,
+            src_ref=ref,
+            dst_ref=ref,
+            send_sem=ring_send.at[index],
+            recv_sem=ring_recv.at[index],
+            device_id={"block": block},
+            device_id_type=MESH,
         )
 
-    first = [push(position, upper, 0, right), push(position, lower, 1, left)]
-    second = [push(position, lower, 2, right), push(position, upper, 3, left)]
-    for copy in first + second:
+    def system(owner, lower):
+        return x_ref.at[owner, :, pl.ds(64 * lower, 64), :]
+
+    early = [push(system(position, 0), 0, right), push(system(position, 1), 1, left)]
+    late = [push(system(position, 1), 2, right), push(system(position, 0), 3, left)]
+    onward = [push(system(left, 0), 4, right), push(system(right, 1), 5, left)]
+    couplings = [push(k_ref.at[position], 6 + i, block) for i, block in enumerate((right, opposite, left))]
+    for copy in early + late:
         copy.start()
-    onward = [push(left, upper, 4, right), push(right, lower, 5, left)]
-    for copy, following in zip(first, onward):
+    for copy, following in zip(early, onward):
         copy.wait_recv()
         following.start()
-    for copy in first:
+    for copy in couplings:
+        copy.start()
+    for copy in early:
         copy.wait_send()
-    for copy in second + onward:
+    for copy in late + onward:
         copy.wait()
+
+    def couplings_arrived():
+        for copy in couplings:
+            copy.wait()
+
+    green = solve(position, x_ref, k_ref, couplings_arrived)
+    for part in (0, 1):
+        held[part] = green[part].reshape(8, 16, 128)
+        green_ref[part] = green[part]
+    exchange(place, held, mid, padded.at[:, 8:], send, recv, 0)
+    flat = padded.reshape(2, 2 * energies, 128)
+    result = done.reshape(2, energies, 128)
+
+    def polarize(w, carry):
+        start = energies - offsets_ref[w]
+        mr, mi = flat[0, pl.ds(start, energies), :], flat[1, pl.ds(start, energies), :]
+        vr, vi = flat[0, energies:, :], flat[1, energies:, :]
+        polar[0, pl.ds(w, 1), :] = factor * jnp.sum(vr * mr - vi * mi, axis=0, keepdims=True)
+        polar[1, pl.ds(w, 1), :] = factor * jnp.sum(vr * mi + vi * mr, axis=0, keepdims=True)
+        return carry
+
+    lax.fori_loop(0, count, polarize, 0)
+    weight = coulomb_ref[...] * tile_row(tiles_ref, 1, (2 * e + c) // TILE, 1, 128)
+    scale = weight * weight * (1.0 / count)
+    rows = 64
+    for n in range(0, energies, rows):
+
+        def interact(w, total):
+            start = energies - offsets_ref[w] + n
+            mr, mi = flat[0, pl.ds(start, rows), :], flat[1, pl.ds(start, rows), :]
+            pr, pi = polar[0, pl.ds(w, 1), :], polar[1, pl.ds(w, 1), :]
+            return total[0] + (mr * pr - mi * pi), total[1] + (mr * pi + mi * pr)
+
+        zero = jnp.zeros((rows, 128), F32)
+        tr, ti = lax.fori_loop(0, count, interact, (zero, zero))
+        result[0, n : n + rows] = tr * scale
+        result[1, n : n + rows] = ti * scale
+    exchange(place, done, mid_back, o_ref, send, recv, 48)
 
 
 def in_vmem():
@@ -344,46 +386,33 @@
 def body(sigma_in, hamiltonian, coupling, coulomb, pattern, offsets):
     width = hamiltonian.shape[-1]
     count = offsets.shape[0]
-    every = pl.pallas_call(
-        gather_kernel,
-        out_shape=jax.ShapeDtypeStruct((4, 3, width, width), F32),
-        in_specs=[pl.BlockSpec(memory_space=pl.ANY)] * 4,
-        out_specs=in_vmem(),
+    planes = (2, 8, 16, width)
+    green, screened = pl.pallas_call(
+        functools.partial(whole_kernel, count),
+        out_shape=[jax.ShapeDtypeStruct((2, width, width), F32), jax.ShapeDtypeStruct(planes, F32)],
+        in_specs=[in_smem()] + [pl.BlockSpec(memory_space=pl.ANY)] * 5,
+        out_specs=[in_vmem()] * 2,
         scratch_shapes=[
             pltpu.SMEM(pattern.shape, pattern.dtype),
             pltpu.VMEM(sigma_in.shape, F32),
             pltpu.VMEM(hamiltonian.shape, F32),
-            pltpu.VMEM(coupling.shape, F32),
-            pltpu.SemaphoreType.DMA((4,)),
-            pltpu.SemaphoreType.DMA((6,)),
-            pltpu.SemaphoreType.DMA((6,)),
-        ],
-        compiler_params=pltpu.CompilerParams(collective_id=2, has_side_effects=True, vmem_limit_bytes=66_180_000),
-    )(pattern, sigma_in, hamiltonian, coupling)
-    green, again = pl.pallas_call(
-        solve_kernel,
-        out_shape=[jax.ShapeDtypeStruct((2, width, width), F32)] * 2,
-        in_specs=[in_vmem()],
-        out_specs=[in_vmem()] * 2,
-        compiler_params=pltpu.CompilerParams(vmem_limit_bytes=24 << 20),
-    )(every)
-    planes = (2, 8, 16, width)
-    screened = pl.pallas_call(
-        functools.partial(screen_kernel, count),
-        out_shape=jax.ShapeDtypeStruct(planes, F32),
-        in_specs=[in_smem(), in_smem(), in_vmem(), in_vmem()],
-        out_specs=in_vmem(),
-        scratch_shapes=[
+            pltpu.VMEM(coulomb.shape, F32),
+            pltpu.VMEM((4, 2, width, width), F32),
+            pltpu.VMEM((4, width, width), F32),
+            pltpu.VMEM(planes, F32),
             pltpu.VMEM(planes, F32),
             pltpu.VMEM((2, 16, 16, width), F32),
             pltpu.VMEM((2, count, width), F32),
             pltpu.VMEM(planes, F32),
             pltpu.VMEM(planes, F32),
+            pltpu.SemaphoreType.DMA((5,)),
+            pltpu.SemaphoreType.DMA((9,)),
+            pltpu.SemaphoreType.DMA((9,)),
             pltpu.SemaphoreType.DMA((96,)),
             pltpu.SemaphoreType.DMA((96,)),
         ],
-        compiler_params=pltpu.CompilerParams(collective_id=1, has_side_effects=True, vmem_limit_bytes=8 << 20),
-    )(offsets, pattern, again.reshape(planes), coulomb)
+        compiler_params=pltpu.CompilerParams(collective_id=1, has_side_effects=True, vmem_limit_bytes=66_600_000),
+    )(offsets, pattern, sigma_in, hamiltonian, coupling, coulomb)
     spread = (2, 1, 1, width, width)
     return green.reshape(spread), screened.reshape(spread)
 

time: 76.1 us -> 71.4 us (0.938)
  Pallas kernels: 72.7 us -> 68.3 us
    pallas_call x3 -> x1, Pallas kernels: 72.7 us -> 68.3 us  [body(): pl.pallas_call(functools.partial(whole_kernel, count), out_shape=[jax.Sha...]
    unnamed x9 -> x4, local copies, waits for them, and re-layouts: 2.47 us -> 2.26 us
where the time goes in v3:
time: 71.4 us; the launch traced here: 71.2 us
  Pallas kernels  68.3 us (96%)
  local copies, waits for them, and re-layouts  2.26 us (3%)
    pallas_call x1, Pallas kernels, body(): pl.pallas_call(functools.partial(whole_kernel, count), out_shape=[jax.Sha...  68.3 us
    unnamed x4, local copies, waits for them, and re-layouts  2.26 us

profile of v3, /device:TPU:1, one launch (start us, length us, event | category | flops | bytes accessed | tf_op | source)
XLA Modules:
  0.0 71.2 jit_solution(11480728026039145837)
XLA Ops:
  0.6 68.3 %shard_map.77 = (f32[2,128,128]{2,1,0:T(8,128)}, f32[2,8,16,128]{3,2,1,0:T(8,128)}) custom-call(s32[16]{0:T(128)} %offsets_ref.1, s32[2,1,4,4]{3,2,1,0:T(4,128)} %tiles.1, f32[2,1,1,128,128]{4,3,2,1,0:T(8,128)} %sigma.1, f32[1,128,128]{2,1,0:T(8,128)} %hamiltonian.1, f32[1,128,128]{2,1,0:T(8,128)} %coupling.1, f32[1,128]{1,0:T(1,128)} %coulomb.1), custom_call_target="tpu_custom_call" | custom-call | tf_op jit(solution)/shard_map/pallas_call | solution.py:390
  69.0 0.0 copy-start
  69.0 1.6 %copy.12 = f32[2,1,1,128,128]{4,3,2,1,0:T(8,128)} copy(f32[2,1,1,128,128]{4,3,2,1,0:T(8,128)} %bitcast.7) | data formatting | bytes 262144
  70.6 0.0 copy-done
  70.6 0.7 copy.13
Async XLA Ops:
  69.0 1.6 %copy-start = (f32[2,8,16,128]{3,2,1,0:T(8,128)S(1)}, f32[2,8,16,128]{3,2,1,0:T(8,128)}, u32[]{:S(2)}) copy-start(f32[2,8,16,128]{3,2,1,0:T(8,128)} %get-tuple-element.5) | copy-start | bytes 393220

commit v4 on v3

--- a/solution.py
+++ b/solution.py
@@ -166,28 +166,30 @@
     fasts = sorted(range(1, 16), key=lambda s: -min(s, 16 - s))
     slows = sorted(range(1, 8), key=lambda s: -min(s, 8 - s))
     one, two = [], []
+    for s in slows:
+        t, device = slow_partner(s)
+        two.append(push(cur.at[1, t], mid.at[1, slow], 16 + s, device))
     for s in fasts:
         t, device = row_partner(s)
         one.append(push(cur.at[0, :, t, :], mid.at[0, :, fast, :], s, device))
-    for s in slows:
-        t, device = slow_partner(s)
-        two.append(push(cur.at[1, t], mid.at[1, slow], 16 + s, device))
     mid[0, :, pl.ds(fast, 1), :] = cur[0, :, pl.ds(fast, 1), :]
     mid[1, pl.ds(slow, 1)] = cur[1, pl.ds(slow, 1)]
     for copy in two:
-        copy.wait()
+        copy.wait_recv()
     for s in fasts:
         t, device = row_partner(s)
         started.append(push(mid.at[1, :, t, :], out.at[1, :, fast, :], 24 + s, device))
     for copy in one:
-        copy.wait()
+        copy.wait_recv()
     for s in slows:
         t, device = slow_partner(s)
         started.append(push(mid.at[0, t], out.at[0, slow], 40 + s, device))
     out[1, :, pl.ds(fast, 1), :] = mid[1, :, pl.ds(fast, 1), :]
     out[0, pl.ds(slow, 1)] = mid[0, pl.ds(slow, 1)]
     for copy in started:
-        copy.wait()
+        copy.wait_recv()
+    for copy in one + two + started:
+        copy.wait_send()
 
 
 MESH = pl.DeviceIdType.MESH
@@ -331,14 +333,14 @@
         following.start()
     for copy in couplings:
         copy.start()
-    for copy in early:
-        copy.wait_send()
     for copy in late + onward:
-        copy.wait()
+        copy.wait_recv()
 
     def couplings_arrived():
         for copy in couplings:
-            copy.wait()
+            copy.wait_recv()
+        for copy in early + late + onward + couplings:
+            copy.wait_send()
 
     green = solve(position, x_ref, k_ref, couplings_arrived)
     for part in (0, 1):
@@ -356,7 +358,7 @@
         polar[1, pl.ds(w, 1), :] = factor * jnp.sum(vr * mi + vi * mr, axis=0, keepdims=True)
         return carry
 
-    lax.fori_loop(0, count, polarize, 0)
+    lax.fori_loop(0, count, polarize, 0, unroll=4)
     weight = coulomb_ref[...] * tile_row(tiles_ref, 1, (2 * e + c) // TILE, 1, 128)
     scale = weight * weight * (1.0 / count)
     rows = 64
@@ -369,7 +371,7 @@
             return total[0] + (mr * pr - mi * pi), total[1] + (mr * pi + mi * pr)
 
         zero = jnp.zeros((rows, 128), F32)
-        tr, ti = lax.fori_loop(0, count, interact, (zero, zero))
+        tr, ti = lax.fori_loop(0, count, interact, (zero, zero), unroll=4)
         result[0, n : n + rows] = tr * scale
         result[1, n : n + rows] = ti * scale
     exchange(place, done, mid_back, o_ref, send, recv, 48)

time: 71.4 us -> 71.3 us (level)
  no operation moved by 1% of the time
where the time goes in v4:
time: 71.3 us; the launch traced here: 71.1 us
  Pallas kernels  68.2 us (96%)
  local copies, waits for them, and re-layouts  2.26 us (3%)
    pallas_call x1, Pallas kernels, body(): pl.pallas_call(functools.partial(whole_kernel, count), out_shape=[jax.Sha...  68.2 us
    unnamed x4, local copies, waits for them, and re-layouts  2.26 us

profile of v4, /device:TPU:1, one launch (start us, length us, event | category | flops | bytes accessed | tf_op | source)
XLA Modules:
  0.0 71.1 jit_solution(6110665229313414997)
XLA Ops:
  0.6 68.2 %shard_map.77 = (f32[2,128,128]{2,1,0:T(8,128)}, f32[2,8,16,128]{3,2,1,0:T(8,128)}) custom-call(s32[16]{0:T(128)} %offsets_ref.1, s32[2,1,4,4]{3,2,1,0:T(4,128)} %tiles.1, f32[2,1,1,128,128]{4,3,2,1,0:T(8,128)} %sigma.1, f32[1,128,128]{2,1,0:T(8,128)} %hamiltonian.1, f32[1,128,128]{2,1,0:T(8,128)} %coupling.1, f32[1,128]{1,0:T(1,128)} %coulomb.1), custom_call_target="tpu_custom_call" | custom-call | tf_op jit(solution)/shard_map/pallas_call | solution.py:392
  68.8 0.0 copy-start
  68.8 1.6 %copy.12 = f32[2,1,1,128,128]{4,3,2,1,0:T(8,128)} copy(f32[2,1,1,128,128]{4,3,2,1,0:T(8,128)} %bitcast.7) | data formatting | bytes 262144
  70.5 0.0 copy-done
  70.5 0.7 copy.13
Async XLA Ops:
  68.8 1.6 %copy-start = (f32[2,8,16,128]{3,2,1,0:T(8,128)S(1)}, f32[2,8,16,128]{3,2,1,0:T(8,128)}, u32[]{:S(2)}) copy-start(f32[2,8,16,128]{3,2,1,0:T(8,128)} %get-tuple-element.5) | copy-start | bytes 393220
